TPU v7x, 32 devices: a whole 2x2x4 slice. The times are simulated.
32 devices in a mesh: vert: 8 (over z, y), col: 4 (over x, core).
Axes of the slice: x: 2, y: 2, z: 4, core: 2. Of those that a mesh axis runs over, the one named last changes fastest.
Arguments:
- coeffs: bfloat16 [64, 400], P(('vert', 'col')), may hold values from -6 to 6
- shape_basis: bfloat16 [400, 3, 656], P('col', None, 'vert'), may hold values from -0.3125 to 0.3125
- template: float32 [3, 656], P(None, 'vert'), may hold values from -6 to 6
- regressor: float32 [55, 656], P(None, 'vert'), may hold values from -0.5 to 0.5
- quaternions: float32 [64, 4, 55], P(('vert', 'col')), may hold values from -1.5 to 1.5, as said below
- translation: float32 [64, 3], P(('vert', 'col')), may hold values from -6 to 6
- parents: int32 [55], replicated, may hold values from 0 to 53, as said below
- skin_index: int32 [656, 4], P('vert'), may hold values from 0 to 54, all different within a row
- skin_raw: float32 [656, 4], P('vert'), may hold values from 0.1 to 1
Outputs:
- posed_vertices: bfloat16 [64, 3, 656], P(('vert', 'col'))
Inputs may be any that keep to these rules, and one draw needn't show every extreme that they name: parents[0] = 0 and parents[j] < j for j >= 1. `skin_index`: the four joints of a vertex differ. `quaternions`: component 0 lies in [0.5, 1.5].
All inputs are finite; a program needn't handle non-finite values.
Results may differ from a plain program's by a relative error of at most 0.0024.
Values may be sent and summed in bfloat16 or wider, within the bound.
No kernel may reach another device: no remote copies, remote signals or barrier semaphores. Data moves between devices by JAX's collectives and lax.ppermute only.
A program may use at most 64 MiB of HBM per device.

v0:
```python
import jax
import jax.numpy as jnp
from jax import lax
from jax.sharding import PartitionSpec as P


def rotations(quaternions):
    quat_w = jnp.transpose(quaternions[:, 0])
    quat_x = jnp.transpose(quaternions[:, 1])
    quat_y = jnp.transpose(quaternions[:, 2])
    quat_z = jnp.transpose(quaternions[:, 3])
    scale_two = 2.0 / (quat_w * quat_w + quat_x * quat_x + quat_y * quat_y + quat_z * quat_z)
    matrix_rows = [
        [
            1.0 - scale_two * (quat_y * quat_y + quat_z * quat_z),
            scale_two * (quat_x * quat_y - quat_w * quat_z),
            scale_two * (quat_x * quat_z + quat_w * quat_y),
        ],
        [
            scale_two * (quat_x * quat_y + quat_w * quat_z),
            1.0 - scale_two * (quat_x * quat_x + quat_z * quat_z),
            scale_two * (quat_y * quat_z - quat_w * quat_x),
        ],
        [
            scale_two * (quat_x * quat_z - quat_w * quat_y),
            scale_two * (quat_y * quat_z + quat_w * quat_x),
            1.0 - scale_two * (quat_x * quat_x + quat_y * quat_y),
        ],
    ]
    return jnp.stack([jnp.stack(entry, axis=1) for entry in matrix_rows], axis=1)


def kinematics(joints, quaternions, translation, parents):
    joint_total = quaternions.shape[2]
    local_rots = rotations(quaternions)
    places = jnp.transpose(joints, (2, 1, 0))
    glob_rot = jnp.zeros_like(local_rots).at[0].set(local_rots[0])
    glob_pos = jnp.zeros_like(places).at[0].set(places[0] + jnp.transpose(translation))

    def compose(joint, state_pair):
        rot_now, pos_now = state_pair
        parent = lax.dynamic_index_in_dim(parents, joint, 0, keepdims=False)
        parent_rot = lax.dynamic_index_in_dim(rot_now, parent, 0, keepdims=False)
        parent_pos = lax.dynamic_index_in_dim(pos_now, parent, 0, keepdims=False)
        local_rot = lax.dynamic_index_in_dim(local_rots, joint, 0, keepdims=False)
        offset = lax.dynamic_index_in_dim(
            places, joint, 0, keepdims=False
        ) - lax.dynamic_index_in_dim(places, parent, 0, keepdims=False)
        new_rot = jnp.einsum("amc,mbc->abc", parent_rot, local_rot, precision=lax.Precision.HIGHEST)
        new_pos = (
            jnp.einsum("amc,mc->ac", parent_rot, offset, precision=lax.Precision.HIGHEST)
            + parent_pos
        )
        rot_now = lax.dynamic_update_index_in_dim(rot_now, new_rot, joint, 0)
        pos_now = lax.dynamic_update_index_in_dim(pos_now, new_pos, joint, 0)
        return (rot_now, pos_now)

    glob_rot, glob_pos = lax.fori_loop(1, joint_total, compose, (glob_rot, glob_pos))
    correction = glob_pos - jnp.einsum(
        "jamc,jmc->jac", glob_rot, places, precision=lax.Precision.HIGHEST
    )
    frames = jnp.concatenate(
        [glob_rot.reshape(joint_total, 9, glob_rot.shape[3]), correction], axis=1
    )
    return jnp.transpose(frames, (2, 1, 0))


def dense_weights(joint_index, raw_weights, joint_total):
    shares = raw_weights / jnp.sum(raw_weights, axis=1, keepdims=True)
    matches = joint_index[None, :, :] == jnp.arange(joint_total, dtype=jnp.int32)[:, None, None]
    return jnp.sum(
        jnp.where(matches, shares[None, :, :], jnp.zeros_like(shares)[None, :, :]), axis=2
    )


def apply_frames(blended, shaped_wide):
    coords = []
    for axis_out in range(3):
        value = blended[:, 9 + axis_out]
        for axis_in in range(3):
            value = value + blended[:, 3 * axis_out + axis_in] * shaped_wide[:, axis_in]
        coords.append(value)
    return jnp.stack(coords, axis=1)


def body(
    coeffs,
    shape_basis,
    template,
    regressor,
    quaternions,
    translation,
    parents,
    skin_index,
    skin_raw,
):
    joint_total = regressor.shape[0]
    full_basis = lax.all_gather(shape_basis, "col", axis=0, tiled=True)
    components = full_basis.shape[0]
    vert_count = full_basis.shape[2]
    flat_basis = full_basis.reshape(components, 3 * vert_count)
    base_row = template.reshape(1, 3 * vert_count)
    full_shape = (
        jnp.dot(
            lax.all_gather(coeffs, "vert", axis=0, tiled=True),
            flat_basis,
            preferred_element_type=jnp.float32,
        )
        + base_row
    )
    group_count = full_shape.shape[0]
    shaped_three = full_shape.astype(jnp.bfloat16).reshape(group_count, 3, vert_count)
    partial_value = jnp.einsum(
        "cmv,jv->cmj",
        full_shape.reshape(group_count, 3, vert_count),
        regressor,
        precision=lax.Precision.HIGHEST,
    )
    joints = lax.psum_scatter(partial_value, "vert", scatter_dimension=0, tiled=True)
    own_frames = kinematics(joints, quaternions, translation, parents)
    group_frames = lax.all_gather(own_frames, "vert", axis=0, tiled=True)
    weight_grid = dense_weights(skin_index, skin_raw, joint_total)
    blended = jnp.einsum("cej,jv->cev", group_frames, weight_grid, precision=lax.Precision.HIGHEST)
    posed_local = apply_frames(blended, shaped_three.astype(jnp.float32)).astype(jnp.bfloat16)
    return lax.all_to_all(posed_local, "vert", split_axis=0, concat_axis=2, tiled=True)


def solution(mesh):
    in_specs = (
        P(("vert", "col"), None),
        P("col", None, "vert"),
        P(None, "vert"),
        P(None, "vert"),
        P(("vert", "col"), None, None),
        P(("vert", "col"), None),
        P(),
        P("vert", None),
        P("vert", None),
    )
    out_specs = P(("vert", "col"), None, None)
    return jax.shard_map(body, mesh=mesh, in_specs=in_specs, out_specs=out_specs, check_vma=False)
```

profile of v0, /device:TPU:0, one launch (start us, length us, event | category | flops | bytes accessed | tf_op | source)
XLA Modules:
  0.0 288.7 jit_solution(18105276202222392193)
XLA Ops:
  0.0 0.9 multiply_add_fusion.2
  0.9 0.8 add.183
  1.7 28.1 %all-gather = bf16[8,2,400]{2,1,0:T(2,128)(2,1)S(1)} all-gather(bf16[1,2,400]{2,1,0:T(2,128)(2,1)} %bitcast.166), channel_id=1, replica_groups=mesh['vert'=8,'col'=4] {'vert'}, dimensions={0}, use_global_device_ids=true | all-gather | bytes 14400 | tf_op jit(solution)/shard_map/all_gather | solution.py:105
  29.9 6.5 %all_gather.10 = bf16[400,3,82]{2,1,0:T(4,128)(2,1)S(1)} all-gather(bf16[100,3,82]{2,1,0:T(4,128)(2,1)S(1)} %copy.86), channel_id=1, replica_groups=mesh['vert'=8,'col'=4] {'col'}, dimensions={0}, use_global_device_ids=true | all-gather | bytes 246000 | tf_op jit(solution)/shard_map/all_gather | solution.py:98
  38.1 35.4 %all-reduce.1 = f32[16,3,55]{2,0,1:T(8,128)S(1)} all-reduce(f32[16,3,55]{2,0,1:T(8,128)S(1)} %fusion.8), channel_id=2, replica_groups=mesh['vert'=8,'col'=4] {'vert'}, use_global_device_ids=true, to_apply=%region_0.0.clone | all-reduce | flops 2640 | bytes 21120
  73.6 0.7 copy-done.8
  77.1 169.4 %while.19 = (s32[]{:T(128)}, f32[55,3,3,2]{2,3,1,0:T(2,128)S(1)}, f32[55,3,2]{1,2,0:T(2,128)S(1)}, f32[55,3,3,2]{2,3,1,0:T(2,128)S(1)}, s32[55]{0:T(128)S(1)}, /...) while((s32[]{:T(128)}, f32[55,3,3,2]{2,3,1,0:T(2,128)S(1)}, ...), condition=%wide.region_2.0_spmd, body=%wide.region_1.0_spmd.sunk | while | flops 884 | bytes 9465 | solution.py:58
  83.3 0.7 dynamic_slice.89
  89.6 0.7 dynamic_slice.89
  95.9 0.7 dynamic_slice.89
  105.3 0.7 dynamic_slice.89
  111.6 0.7 dynamic_slice.89
  117.8 0.7 dynamic_slice.89
  124.1 0.7 dynamic_slice.89
  127.3 0.7 dynamic_slice.89
  133.5 0.7 dynamic_slice.89
  139.8 0.7 dynamic_slice.89
  146.1 0.7 dynamic_slice.89
  155.5 0.7 dynamic_slice.89
  161.8 0.7 dynamic_slice.89
  168.0 0.7 dynamic_slice.89
  174.3 0.7 dynamic_slice.89
  177.5 0.7 dynamic_slice.89
  183.7 0.7 dynamic_slice.89
  190.0 0.7 dynamic_slice.89
  196.3 0.7 dynamic_slice.89
  224.5 0.7 dynamic_slice.89
  240.2 0.7 dynamic_slice.89
  247.3 30.5 %all_gather.11 = f32[16,12,55]{2,1,0:T(8,128)S(1)} all-gather(f32[2,12,55]{2,1,0:T(8,128)S(1)} %copy.95), channel_id=1, replica_groups=mesh['vert'=8,'col'=4] {'vert'}, dimensions={0}, use_global_device_ids=true | all-gather | bytes 47520 | tf_op jit(solution)/shard_map/all_gather | solution.py:121
  277.9 0.7 copy-done.4
  279.0 8.9 %all_to_all.18 = bf16[8,2,246]{2,1,0:T(2,128)(2,1)S(1)} all-to-all(bf16[8,2,246]{2,1,0:T(2,128)(2,1)S(1)} %reshape.121), channel_id=1, replica_groups=mesh['vert'=8,'col'=4] {'vert'}, dimensions={0} | all-to-all | bytes 15744 | tf_op jit(solution)/shard_map/all_to_all | solution.py:125
  288.0 0.7 all_to_all.16
  (575 shorter events, 58.8 us)
Async XLA Ops:
  0.0 38.0 %copy-start = (f32[55,82]{1,0:T(8,128)S(1)}, f32[55,82]{1,0:T(8,128)}, u32[]{:S(2)}) copy-start(f32[55,82]{1,0:T(8,128)} %param.18) | copy-start | bytes 54124
  0.0 0.9 copy-start.2
  0.0 29.8 %copy-start.1 = (bf16[100,3,82]{0,2,1:T(8,128)(2,1)S(1)}, bf16[100,3,82]{0,2,1:T(8,128)(2,1)}, u32[]{:S(2)}) copy-start(bf16[100,3,82]{0,2,1:T(8,128)(2,1)} %param.16) | copy-start | bytes 147604
  37.0 0.7 copy-start.6
  73.6 0.7 copy-start.8
  75.7 0.7 copy-start.5
  76.4 0.7 copy-start.7
  247.3 30.6 %copy-start.3 = (f32[82,4]{0,1:T(4,128)S(1)}, f32[82,4]{0,1:T(4,128)}, u32[]{:S(2)}) copy-start(f32[82,4]{0,1:T(4,128)} %param.23) | copy-start | bytes 3940
  277.9 0.7 copy-start.4
where the time goes:
time: 291 us; the launch traced here: 289 us
  blocking collectives  109 us (37%)
  loops' own time  102 us (35%)
  local copies, waits for them, and re-layouts  54.8 us (19%)
  matrix products  19.3 us (7%)
    another operation x1, loops' own time, kinematics(): lax.fori_loop(1, joint_total, compose, (glob_rot, glob_pos))  102 us
    unnamed x1, blocking collectives  35.4 us
    dynamic_slice x54, local copies, waits for them, and re-layouts, compose(): parent = lax.dynamic_index_in_dim(parents, joint, 0, keepdims=False)  35.1 us
    all_gather x1, blocking collectives, body(): group_frames = lax.all_gather(own_frames, 'vert', axis=0, tiled=True)  30.5 us
    all_gather x1, blocking collectives, body(): lax.all_gather(coeffs, 'vert', axis=0, tiled=True)  28.1 us
    dot_general x54, matrix products, compose(): jnp.einsum('amc,mbc->abc', parent_rot, local_rot, precision=lax.Precision...  11.1 us
    all_to_all x1, blocking collectives, body(): lax.all_to_all(posed_local, 'vert', split_axis=0, concat_axis=2, tiled=True)  8.89 us
    dot_general x54, matrix products, compose(): jnp.einsum('amc,mc->ac', parent_rot, offset, precision=lax.Precision.HIGH...  7.68 us

commit v1 on v0

--- a/solution.py
+++ b/solution.py
@@ -118,9 +118,20 @@
     )
     joints = lax.psum_scatter(partial_value, "vert", scatter_dimension=0, tiled=True)
     own_frames = kinematics(joints, quaternions, translation, parents)
-    group_frames = lax.all_gather(own_frames, "vert", axis=0, tiled=True)
     weight_grid = dense_weights(skin_index, skin_raw, joint_total)
-    blended = jnp.einsum("cej,jv->cev", group_frames, weight_grid, precision=lax.Precision.HIGHEST)
+    size, here, rows = (lax.axis_size("vert"), lax.axis_index("vert"), own_frames.shape[0])
+    right = [(i, (i + 1) % size) for i in range(size)]
+    block, out = (own_frames, None)
+    for lap in range(size):
+        source = (here - lap) % size
+        coming = lax.ppermute(block, "vert", right) if lap < size - 1 else None
+        made = jnp.einsum("cej,jv->cev", block, weight_grid, precision=lax.Precision.HIGHEST)
+        length = made.shape[0]
+        if out is None:
+            out = jnp.zeros((*made.shape[:0], size * length, *made.shape[0 + 1 :]), made.dtype)
+        out = lax.dynamic_update_slice_in_dim(out, made, source * length, axis=0)
+        block = coming
+    blended = out
     posed_local = apply_frames(blended, shaped_three.astype(jnp.float32)).astype(jnp.bfloat16)
     return lax.all_to_all(posed_local, "vert", split_axis=0, concat_axis=2, tiled=True)
 

time: 291 us -> 287 us (0.986)
  waiting for transfers between devices: 0 us -> 42.4 us
  blocking collectives: 109 us -> 78.9 us
  loops' own time: 102 us -> 89.4 us
  local copies, waits for them, and re-layouts: 54.8 us -> 51.4 us
    ppermute x0 -> x7, waiting for transfers between devices: none -> 42.4 us  [body(): coming = lax.ppermute(block, 'vert', right) if lap < size - 1 else None]
    all_gather x1 -> x0, blocking collectives: 30.5 us -> none  [body(): group_frames = lax.all_gather(own_frames, 'vert', axis=0, tiled=True)]
    another operation x1, loops' own time: 102 us -> 89.4 us  [kinematics(): lax.fori_loop(1, joint_total, compose, (glob_rot, glob_pos))]
    dynamic_slice x54, local copies, waits for them, and re-layouts: 35.1 us -> 30.7 us  [compose(): parent = lax.dynamic_index_in_dim(parents, joint, 0, keepdims=False)]
    unnamed x25 -> x29, local copies, waits for them, and re-layouts: 4.25 us -> 5.93 us
  transfers between devices with their start and end apart: 0 -> 7, of which waited for: 0 -> 7; matrix products, arithmetic and copies ran while one was open for 0% -> 0% of each run, Pallas kernels for 0% -> 0%
where the time goes in v1:
time: 287 us; the launch traced here: 285 us
  loops' own time  89.4 us (31%)
  blocking collectives  78.9 us (27%)
  local copies, waits for them, and re-layouts  51.4 us (18%)
  waiting for transfers between devices  42.4 us (15%)
  matrix products  20.2 us (7%)
    another operation x1, loops' own time, kinematics(): lax.fori_loop(1, joint_total, compose, (glob_rot, glob_pos))  89.4 us
    ppermute x7, waiting for transfers between devices, body(): coming = lax.ppermute(block, 'vert', right) if lap < size - 1 else None  42.4 us
    unnamed x1, blocking collectives  35.6 us
    dynamic_slice x54, local copies, waits for them, and re-layouts, compose(): parent = lax.dynamic_index_in_dim(parents, joint, 0, keepdims=False)  30.7 us
    all_gather x1, blocking collectives, body(): lax.all_gather(coeffs, 'vert', axis=0, tiled=True)  27.9 us
    dot_general x54, matrix products, compose(): jnp.einsum('amc,mbc->abc', parent_rot, local_rot, precision=lax.Precision...  11.1 us
    all_to_all x1, blocking collectives, body(): lax.all_to_all(posed_local, 'vert', split_axis=0, concat_axis=2, tiled=True)  8.89 us
    dot_general x54, matrix products, compose(): jnp.einsum('amc,mc->ac', parent_rot, offset, precision=lax.Precision.HIGH...  7.68 us
  transfers between devices with their start and end apart: 7, of which 7 were waited for; matrix products, arithmetic and copies ran while one was open for 0% of the time, Pallas kernels for 0%

profile of v1, /device:TPU:0, one launch (start us, length us, event | category | flops | bytes accessed | tf_op | source)
XLA Modules:
  0.0 285.4 jit_solution(461130200804928822)
XLA Ops:
  0.0 0.9 multiply_add_fusion.2
  1.0 0.6 copy-done.8
  2.4 0.6 copy-done.4
  3.0 27.9 %all-gather = bf16[8,2,400]{2,1,0:T(2,128)(2,1)S(1)} all-gather(bf16[1,2,400]{2,1,0:T(2,128)(2,1)S(1)} %bitcast.182), channel_id=1, replica_groups=mesh['vert'=8,'col'=4] {'vert'}, dimensions={0}, use_global_device_ids=true | all-gather | bytes 14400 | tf_op jit(solution)/shard_map/all_gather | solution.py:105
  31.1 6.5 %all_gather.7 = bf16[400,3,82]{2,1,0:T(4,128)(2,1)S(1)} all-gather(bf16[100,3,82]{2,1,0:T(4,128)(2,1)S(1)} %copy.56), channel_id=1, replica_groups=mesh['vert'=8,'col'=4] {'col'}, dimensions={0}, use_global_device_ids=true | all-gather | bytes 246000 | tf_op jit(solution)/shard_map/all_gather | solution.py:98
  38.3 35.6 %all-reduce.1 = f32[16,3,55]{2,0,1:T(8,128)S(1)} all-reduce(f32[16,3,55]{2,0,1:T(8,128)S(1)} %fusion.13), channel_id=2, replica_groups=mesh['vert'=8,'col'=4] {'vert'}, use_global_device_ids=true, to_apply=%region_0.0.clone | all-reduce | flops 2640 | bytes 21120
  73.9 0.7 copy-done.10
  76.6 0.6 copy-done.9
  77.2 152.1 %while.19 = (s32[]{:T(128)}, f32[55,3,3,2]{2,3,1,0:T(2,128)S(1)}, f32[55,3,2]{1,2,0:T(2,128)S(1)}, f32[55,3,3,2]{2,3,1,0:T(2,128)S(1)}, s32[55]{0:T(128)S(1)}, /...) while((s32[]{:T(128)}, f32[55,3,3,2]{2,3,1,0:T(2,128)S(1)}, ...), condition=%wide.region_2.0_spmd, body=%wide.region_1.0_spmd.sunk | while | flops 884 | bytes 9465 | solution.py:58
  80.0 0.6 dynamic_slice.89
  88.5 0.6 dynamic_slice.89
  94.1 0.6 dynamic_slice.89
  99.7 0.6 dynamic_slice.89
  105.4 0.6 dynamic_slice.89
  108.2 0.6 dynamic_slice.89
  113.8 0.6 dynamic_slice.89
  119.5 0.6 dynamic_slice.89
  125.1 0.6 dynamic_slice.89
  133.5 0.6 dynamic_slice.89
  139.2 0.6 dynamic_slice.89
  144.8 0.6 dynamic_slice.89
  230.2 0.7 copy-done.3
  231.0 0.7 copy-done.5
  232.1 4.6 %collective-permute-done = f32[2,12,55]{2,1,0:T(8,128)S(1)} collective-permute-done((f32[2,12,55]{2,1,0:T(8,128)S(1)}, f32[2,12,55]{2,1,0:T(8,128)S(1)}, u32[]{:S(2)}, u32[]{:S(2)}) %collective-permute-start) | collective-permute-done | bytes 5312 | tf_op jit(solution)/shard_map/ppermute | solution.py:127
  236.7 6.3 %collective-permute-done.1 = f32[2,12,55]{2,1,0:T(8,128)S(1)} collective-permute-done((f32[2,12,55]{2,1,0:T(8,128)S(1)}, f32[2,12,55]{2,1,0:T(8,128)S(1)}, u32[]{:S(2)}, u32[]{:S(2)}) %collective-permute-start.1) | collective-permute-done | bytes 5312 | tf_op jit(solution)/shard_map/ppermute | solution.py:127
  243.2 6.3 %collective-permute-done.2 = f32[2,12,55]{2,1,0:T(8,128)S(1)} collective-permute-done((f32[2,12,55]{2,1,0:T(8,128)S(1)}, f32[2,12,55]{2,1,0:T(8,128)S(1)}, u32[]{:S(2)}, u32[]{:S(2)}) %collective-permute-start.2) | collective-permute-done | bytes 5312 | tf_op jit(solution)/shard_map/ppermute | solution.py:127
  249.6 6.3 %collective-permute-done.3 = f32[2,12,55]{2,1,0:T(8,128)S(1)} collective-permute-done((f32[2,12,55]{2,1,0:T(8,128)S(1)}, f32[2,12,55]{2,1,0:T(8,128)S(1)}, u32[]{:S(2)}, u32[]{:S(2)}) %collective-permute-start.3) | collective-permute-done | bytes 5312 | tf_op jit(solution)/shard_map/ppermute | solution.py:127
  256.1 6.3 %collective-permute-done.4 = f32[2,12,55]{2,1,0:T(8,128)S(1)} collective-permute-done((f32[2,12,55]{2,1,0:T(8,128)S(1)}, f32[2,12,55]{2,1,0:T(8,128)S(1)}, u32[]{:S(2)}, u32[]{:S(2)}) %collective-permute-start.4) | collective-permute-done | bytes 5312 | tf_op jit(solution)/shard_map/ppermute | solution.py:127
  262.5 6.3 %collective-permute-done.5 = f32[2,12,55]{2,1,0:T(8,128)S(1)} collective-permute-done((f32[2,12,55]{2,1,0:T(8,128)S(1)}, f32[2,12,55]{2,1,0:T(8,128)S(1)}, u32[]{:S(2)}, u32[]{:S(2)}) %collective-permute-start.5) | collective-permute-done | bytes 5312 | tf_op jit(solution)/shard_map/ppermute | solution.py:127
  268.9 6.3 %collective-permute-done.6 = f32[2,12,55]{2,1,0:T(8,128)S(1)} collective-permute-done((f32[2,12,55]{2,1,0:T(8,128)S(1)}, f32[2,12,55]{2,1,0:T(8,128)S(1)}, u32[]{:S(2)}, u32[]{:S(2)}) %collective-permute-start.6) | collective-permute-done | bytes 5312 | tf_op jit(solution)/shard_map/ppermute | solution.py:127
  275.7 8.9 %all_to_all.18 = bf16[8,2,246]{2,1,0:T(2,128)(2,1)S(1)} all-to-all(bf16[8,2,246]{2,1,0:T(2,128)(2,1)S(1)} %reshape.121), channel_id=1, replica_groups=mesh['vert'=8,'col'=4] {'vert'}, dimensions={0} | all-to-all | bytes 15744 | tf_op jit(solution)/shard_map/all_to_all | solution.py:136
  284.7 0.7 all_to_all.16
  (599 shorter events, 61.5 us)
Async XLA Ops:
  0.0 38.1 %copy-start = (f32[55,82]{1,0:T(8,128)S(1)}, f32[55,82]{1,0:T(8,128)}, u32[]{:S(2)}) copy-start(f32[55,82]{1,0:T(8,128)} %param.18) | copy-start | bytes 54124
  0.0 0.9 copy-start.2
  1.0 0.7 copy-start.8
  1.7 0.7 copy-start.6
  1.7 29.3 %copy-start.1 = (bf16[100,3,82]{0,2,1:T(8,128)(2,1)S(1)}, bf16[100,3,82]{0,2,1:T(8,128)(2,1)}, u32[]{:S(2)}) copy-start(bf16[100,3,82]{0,2,1:T(8,128)(2,1)} %param.16) | copy-start | bytes 147604
  2.3 0.7 copy-start.4
  73.9 0.7 copy-start.10
  75.9 0.7 copy-start.7
  76.6 0.7 copy-start.9
  230.1 6.5 %collective-permute-start = (f32[2,12,55]{2,1,0:T(8,128)S(1)}, f32[2,12,55]{2,1,0:T(8,128)S(1)}, u32[]{:S(2)}, u32[]{:S(2)}) collective-permute-start(f32[2,12,55]{2,1,0:T(8,128)S(1)} %maximum_bitcast_fusion), channel_id=1, source_target_pairs={{0,4},{4,8},{8,12},{12,16},{16,20},{20,24},{24,28},{28,0},{1,5},{5... | collective-permute-start | bytes 15848 | tf_op jit(solution)/shard_map/ppermute | solution.py:127
  230.2 0.7 copy-start.3
  230.9 0.7 copy-start.5
  236.6 6.4 %collective-permute-start.1 = (f32[2,12,55]{2,1,0:T(8,128)S(1)}, f32[2,12,55]{2,1,0:T(8,128)S(1)}, u32[]{:S(2)}, u32[]{:S(2)}) collective-permute-start(f32[2,12,55]{2,1,0:T(8,128)S(1)} %collective-permute-done), channel_id=1, source_target_pairs={{0,4},{4,8},{8,12},{12,16},{16,20},{20,24},{24,28},{28,0},{1,5},{5... | collective-permute-start | bytes 15848 | tf_op jit(solution)/shard_map/ppermute | solution.py:127
  243.0 6.4 %collective-permute-start.2 = (f32[2,12,55]{2,1,0:T(8,128)S(1)}, f32[2,12,55]{2,1,0:T(8,128)S(1)}, u32[]{:S(2)}, u32[]{:S(2)}) collective-permute-start(f32[2,12,55]{2,1,0:T(8,128)S(1)} %collective-permute-done.1), channel_id=1, source_target_pairs={{0,4},{4,8},{8,12},{12,16},{16,20},{20,24},{24,28},{28,0},{1,5},{5... | collective-permute-start | bytes 15848 | tf_op jit(solution)/shard_map/ppermute | solution.py:127
  249.5 6.4 %collective-permute-start.3 = (f32[2,12,55]{2,1,0:T(8,128)S(1)}, f32[2,12,55]{2,1,0:T(8,128)S(1)}, u32[]{:S(2)}, u32[]{:S(2)}) collective-permute-start(f32[2,12,55]{2,1,0:T(8,128)S(1)} %collective-permute-done.2), channel_id=1, source_target_pairs={{0,4},{4,8},{8,12},{12,16},{16,20},{20,24},{24,28},{28,0},{1,5},{5... | collective-permute-start | bytes 15848 | tf_op jit(solution)/shard_map/ppermute | solution.py:127
  255.9 6.4 %collective-permute-start.4 = (f32[2,12,55]{2,1,0:T(8,128)S(1)}, f32[2,12,55]{2,1,0:T(8,128)S(1)}, u32[]{:S(2)}, u32[]{:S(2)}) collective-permute-start(f32[2,12,55]{2,1,0:T(8,128)S(1)} %collective-permute-done.3), channel_id=1, source_target_pairs={{0,4},{4,8},{8,12},{12,16},{16,20},{20,24},{24,28},{28,0},{1,5},{5... | collective-permute-start | bytes 15848 | tf_op jit(solution)/shard_map/ppermute | solution.py:127
  262.4 6.5 %collective-permute-start.5 = (f32[2,12,55]{2,1,0:T(8,128)S(1)}, f32[2,12,55]{2,1,0:T(8,128)S(1)}, u32[]{:S(2)}, u32[]{:S(2)}) collective-permute-start(f32[2,12,55]{2,1,0:T(8,128)S(1)} %collective-permute-done.4), channel_id=1, source_target_pairs={{0,4},{4,8},{8,12},{12,16},{16,20},{20,24},{24,28},{28,0},{1,5},{5... | collective-permute-start | bytes 15848 | tf_op jit(solution)/shard_map/ppermute | solution.py:127
  268.8 6.4 %collective-permute-start.6 = (f32[2,12,55]{2,1,0:T(8,128)S(1)}, f32[2,12,55]{2,1,0:T(8,128)S(1)}, u32[]{:S(2)}, u32[]{:S(2)}) collective-permute-start(f32[2,12,55]{2,1,0:T(8,128)S(1)} %collective-permute-done.5), channel_id=1, source_target_pairs={{0,4},{4,8},{8,12},{12,16},{16,20},{20,24},{24,28},{28,0},{1,5},{5... | collective-permute-start | bytes 15848 | tf_op jit(solution)/shard_map/ppermute | solution.py:127
